TPU v7x, 32 devices: a whole 2x2x4 slice. The times are simulated.
32 devices in a mesh: rows: 4 (over x, core), cols: 8 (over z, y).
Axes of the slice: x: 2, y: 2, z: 4, core: 2. Of those that a mesh axis runs over, the one named last changes fastest.
Arguments:
- samples: bfloat16 [2048, 65536], P('rows', 'cols'), may hold values from -0.0234375 to 0.0234375
- labels: int32 [2048], P('rows'), may hold values 0 or 1
- weights: float32 [65536], P('cols'), may hold values from -7 to 7, as said below
- hist_s: float32 [16, 65536], P(None, 'cols'), may hold values from -60 to 60
- hist_y: float32 [16, 65536], P(None, 'cols'), may hold values from -480 to 480, as said below
- counter: int32 [1], replicated, may hold values from 0 to 4095
Outputs:
- new_weights: float32 [65536], P('cols')
- gradient: float32 [65536], P('cols')
Inputs may be any that keep to these rules, and one draw needn't show every extreme that they name: weights share a common direction with the rows of hist_s. Each entry of hist_y[j] is a positive multiple of the same entry of hist_s[j], so s_j . y_j > 0.
All inputs are finite; a program needn't handle non-finite values. No bound on the sum of `labels` on one device may be relied on, other than what follows from the above.
Results may differ from a plain program's by a relative error of at most 0.0013.
Values sent between devices are 32-bit elements; how exact they have to be, the bound alone decides.
A program may use at most 64 MiB of HBM per device.

v0:
```python
import jax
import jax.numpy as jnp
from jax import lax
from jax.sharding import PartitionSpec as P

HIST = 16
penalty = 4.0
step_length = 0.5
highest = lax.Precision.HIGHEST


def row_share(values):
    width = values.shape[-1] // lax.axis_size("rows")
    return lax.dynamic_slice_in_dim(values, lax.axis_index("rows") * width, width, values.ndim - 1)


def quad_form(left, matrix, right):
    return jnp.dot(left, jnp.dot(matrix, right, precision=highest), precision=highest)


def gram_recursion(gram, basis, newest):
    count = 2 * HIST + 1
    places = jnp.arange(count, dtype=jnp.int32)
    select_s = (places == newest).astype(jnp.float32)
    select_y = (places == newest + HIST).astype(jnp.float32)
    gamma = quad_form(select_s, gram, select_y) / quad_form(select_y, gram, select_y)
    weights_of = (places == 2 * HIST).astype(jnp.float32)
    coefs = []
    pairs = []
    for step in range(HIST):
        slot = (newest - step) % HIST
        pick_s = (places == slot).astype(jnp.float32)
        pick_y = (places == slot + HIST).astype(jnp.float32)
        rho = 1.0 / quad_form(pick_s, gram, pick_y)
        coef = rho * quad_form(pick_s, gram, weights_of)
        coefs.append(coef)
        pairs.append((pick_s, pick_y, rho))
        weights_of = weights_of - coef * pick_y
    result_of = gamma * weights_of
    for step in reversed(range(HIST)):
        pick_s, pick_y, rho = pairs[step]
        beta = rho * quad_form(pick_y, gram, result_of)
        result_of = result_of + (coefs[step] - beta) * pick_s
    return jnp.dot(result_of, basis, precision=highest)


def body(samples, labels, weights, hist_s, hist_y, counter):
    margin_part = jnp.dot(samples, weights.astype(jnp.bfloat16), preferred_element_type=jnp.float32)
    margin = lax.psum(margin_part, "cols")
    resid = (jax.nn.sigmoid(margin) - labels.astype(jnp.float32)).astype(jnp.bfloat16)
    total_part = jnp.dot(resid, samples, preferred_element_type=jnp.float32)
    newest = counter[0] % HIST
    total = lax.psum(total_part, "rows")
    gradient = weights + penalty * total
    basis = jnp.concatenate([hist_s, hist_y, gradient[None, :]], axis=0)
    narrow_basis = row_share(basis)
    gram_part = jnp.dot(
        narrow_basis, narrow_basis.T, precision=highest, preferred_element_type=jnp.float32
    )
    gram = lax.psum(gram_part, ("rows", "cols"))
    result = gram_recursion(gram, basis, newest)
    return (weights - step_length * result, gradient)


def solution(mesh):
    in_specs = (P("rows", "cols"), P("rows"), P("cols"), P(None, "cols"), P(None, "cols"), P())
    out_specs = (P("cols"), P("cols"))
    return jax.shard_map(body, mesh=mesh, in_specs=in_specs, out_specs=out_specs, check_vma=False)
```

profile of v0, /device:TPU:14, one launch (start us, length us, event | category | flops | bytes accessed | tf_op | source)
XLA Modules:
  0.0 156.8 jit_solution(8693725162735482173)
XLA Ops:
  0.6 0.8 convert_element_type.8
  1.4 5.6 %fusion.186 = f32[1,512]{1,0:T(1,128)S(1)} fusion(bf16[512,8192]{1,0:T(8,128)(2,1)} %param.6, bf16[8192,1]{0,1:T(2,128)(2,1)S(1)} %reshape.4), kind=kOutput, calls=%fused_computation.303 | convolution fusion | flops 8388608 | bytes 8407040 | tf_op jit(solution)/shard_map/dot_general | solution.py:48
  7.1 15.2 %psum.21 = f32[512]{0:T(512)S(1)} all-reduce(f32[512]{0:T(512)S(1)} %bitcast.507), channel_id=1, replica_groups=mesh['rows'=4,'cols'=8] {'cols'}, use_global_device_ids=true, to_apply=%region_0.0 | all-reduce | flops 512 | bytes 4096 | tf_op jit(solution)/shard_map/psum | solution.py:49
  22.3 4.7 %fusion.187 = f32[1,8192]{1,0:T(1,128)S(1)} fusion(bf16[512,1]{0,1:T(2,128)(2,1)S(1)} %reshape.6, bf16[512,8192]{1,0:T(8,128)(2,1)} %param.6), kind=kOutput, calls=%fused_computation.304 | convolution fusion | flops 8388608 | bytes 8422400 | tf_op jit(solution)/shard_map/dot_general | solution.py:51
  26.9 10.4 %psum.22 = f32[8192]{0:T(1024)S(1)} all-reduce(f32[8192]{0:T(1024)S(1)} %bitcast.505), channel_id=1, replica_groups=mesh['rows'=4,'cols'=8] {'rows'}, use_global_device_ids=true, to_apply=%region_1.2 | all-reduce | flops 8192 | bytes 65536 | tf_op jit(solution)/shard_map/psum | solution.py:53
  37.9 45.6 %psum.23 = f32[33,33]{1,0:T(8,128)S(1)} all-reduce(f32[33,33]{1,0:T(8,128)S(1)} %fusion.96), channel_id=1, replica_groups=mesh['rows'=4,'cols'=8] {'rows','cols'}, use_global_device_ids=true, to_apply=%region_2.3 | all-reduce | flops 1089 | bytes 8712 | tf_op jit(solution)/shard_map/psum | solution.py:60
  85.7 0.7 fusion.49
  87.1 0.7 fusion.50
  88.5 0.8 fusion.51
  90.0 0.7 fusion.52
  91.4 0.8 fusion.53
  92.8 0.7 fusion.56
  94.3 0.7 fusion.54
  95.7 0.8 fusion.55
  97.1 0.8 fusion.57
  98.6 0.7 fusion.60
  100.0 0.7 fusion.58
  101.5 0.8 fusion.59
  102.9 0.8 fusion.61
  107.2 0.8 fusion.63
  108.6 0.8 fusion.65
  110.1 0.7 fusion.68
  111.5 0.7 fusion.66
  113.0 0.8 fusion.67
  114.4 0.8 fusion.69
  115.8 0.7 fusion.72
  118.7 0.8 fusion.71
  120.1 0.8 fusion.73
  124.5 0.8 fusion.75
  125.9 0.8 fusion.77
  128.8 0.8 fusion.79
  130.2 0.8 fusion.121
  132.4 0.8 fusion.80
  133.8 0.8 fusion.81
  135.3 0.8 fusion.82
  136.7 0.8 fusion.83
  138.2 0.8 fusion.84
  139.6 0.8 fusion.85
  141.1 0.8 fusion.86
  142.5 0.8 fusion.87
  144.0 0.8 fusion.88
  145.4 0.8 fusion.89
  146.9 0.8 fusion.90
  148.3 0.8 fusion.91
  149.8 0.8 fusion.92
  151.2 0.8 fusion.93
  152.6 0.8 fusion.94
  154.0 0.8 fusion.95
  (39 shorter events, 7.7 us)
Async XLA Ops:
  1.4 20.8 %copy-start.4 = (s32[512]{0:T(512)S(1)}, s32[512]{0:T(512)}, u32[]{:S(2)}) copy-start(s32[512]{0:T(512)} %param.7) | copy-start | bytes 6148
  22.2 15.1 %copy-start.2 = (f32[8192]{0:T(1024)S(1)}, f32[8192]{0:T(1024)}, u32[]{:S(2)}) copy-start(f32[8192]{0:T(1024)} %param.8) | copy-start | bytes 98308
  22.3 15.1 %copy-start = (f32[16,8192]{1,0:T(8,128)S(1)}, f32[16,8192]{1,0:T(8,128)}, u32[]{:S(2)}) copy-start(f32[16,8192]{1,0:T(8,128)} %param.10) | copy-start | bytes 1572868
  22.3 15.1 %copy-start.1 = (f32[16,8192]{1,0:T(8,128)S(1)}, f32[16,8192]{1,0:T(8,128)}, u32[]{:S(2)}) copy-start(f32[16,8192]{1,0:T(8,128)} %param.9) | copy-start | bytes 1572868
  37.4 118.1 %copy-start.3 = (f32[8192]{0:T(1024)}, f32[8192]{0:T(1024)S(1)}, u32[]{:S(2)}) copy-start(f32[8192]{0:T(1024)S(1)} %multiply_add_fusion) | copy-start | bytes 98308
where the time goes:
time: 158 us; the launch traced here: 157 us
  blocking collectives  71.2 us (45%)
  matrix products  48.3 us (31%)
  between operations  35.2 us (22%)
  other arithmetic  2.05 us (1%)
    psum x1, blocking collectives, body(): gram = lax.psum(gram_part, ('rows', 'cols'))  45.6 us
    dot_general x49, matrix products, quad_form(): jnp.dot(matrix, right, precision=highest)  36.8 us
    psum x1, blocking collectives, body(): margin = lax.psum(margin_part, 'cols')  15.2 us
    psum x1, blocking collectives, body(): total = lax.psum(total_part, 'rows')  10.4 us
    dot_general x1, matrix products, body(): jnp.dot(samples, weights.astype(jnp.bfloat16), preferred_element_type=jnp...  5.64 us
    dot_general x1, matrix products, body(): total_part = jnp.dot(resid, samples, preferred_element_type=jnp.float32)  4.66 us

commit v1 on v0

--- a/solution.py
+++ b/solution.py
@@ -46,7 +46,8 @@
 
 def body(samples, labels, weights, hist_s, hist_y, counter):
     margin_part = jnp.dot(samples, weights.astype(jnp.bfloat16), preferred_element_type=jnp.float32)
-    margin = lax.psum(margin_part, "cols")
+    page_start = lambda local: jax.lax.all_gather(local, "cols").sum(axis=0)
+    margin = page_start(margin_part)
     resid = (jax.nn.sigmoid(margin) - labels.astype(jnp.float32)).astype(jnp.bfloat16)
     total_part = jnp.dot(resid, samples, preferred_element_type=jnp.float32)
     newest = counter[0] % HIST

time: 158 us -> 164 us (1.038)
  blocking collectives: 71.2 us -> 76 us
    all_gather x0 -> x1, blocking collectives: none -> 25.2 us  [body(): page_start = lambda local: jax.lax.all_gather(local, 'cols').sum(axis=0)]
    psum x1 -> x0, blocking collectives: 15.2 us -> none  [body(): margin = lax.psum(margin_part, 'cols')]
    psum x1, blocking collectives: 45.6 us -> 40.4 us  [body(): gram = lax.psum(gram_part, ('rows', 'cols'))]
where the time goes in v1:
time: 164 us; the launch traced here: 162 us
  blocking collectives  76 us (46%)
  matrix products  48.3 us (29%)
  between operations  35.3 us (22%)
  other arithmetic  2.08 us (1%)
    psum x1, blocking collectives, body(): gram = lax.psum(gram_part, ('rows', 'cols'))  40.4 us
    dot_general x49, matrix products, quad_form(): jnp.dot(matrix, right, precision=highest)  36.8 us
    all_gather x1, blocking collectives, body(): page_start = lambda local: jax.lax.all_gather(local, 'cols').sum(axis=0)  25.2 us
    psum x1, blocking collectives, body(): total = lax.psum(total_part, 'rows')  10.4 us
    dot_general x1, matrix products, body(): jnp.dot(samples, weights.astype(jnp.bfloat16), preferred_element_type=jnp...  5.64 us
    dot_general x1, matrix products, body(): total_part = jnp.dot(resid, samples, preferred_element_type=jnp.float32)  4.66 us

profile of v1, /device:TPU:14, one launch (start us, length us, event | category | flops | bytes accessed | tf_op | source)
XLA Modules:
  0.0 161.6 jit_solution(2406613836114162533)
XLA Ops:
  0.6 0.8 convert_element_type.8
  1.4 5.6 %convolution_bitcast_fusion = f32[1,1,512]{2,1,0:T(1,128)S(1)} fusion(bf16[512,8192]{1,0:T(8,128)(2,1)} %param.6, bf16[8192,1]{0,1:T(2,128)(2,1)S(1)} %reshape.8), kind=kOutput, calls=%fused_computation.1 | convolution fusion | flops 8388608 | bytes 8407040 | tf_op jit(solution)/shard_map/dot_general | solution.py:48
  7.1 25.2 %all-gather.1 = f32[8,1,512]{2,1,0:T(1,128)S(1)} all-gather(f32[1,1,512]{2,1,0:T(1,128)S(1)} %convolution_bitcast_fusion), channel_id=2, replica_groups=mesh['rows'=4,'cols'=8] {'cols'}, dimensions={0}, use_global_device_ids=true | all-gather | bytes 18432 | tf_op jit(solution)/shard_map/all_gather | solution.py:49
  32.3 4.7 %fusion.186 = f32[1,8192]{1,0:T(1,128)S(1)} fusion(bf16[512,1]{0,1:T(2,128)(2,1)S(1)} %reshape.10, bf16[512,8192]{1,0:T(8,128)(2,1)} %param.6), kind=kOutput, calls=%fused_computation.304 | convolution fusion | flops 8388608 | bytes 8422400 | tf_op jit(solution)/shard_map/dot_general | solution.py:52
  37.0 10.4 %psum.14 = f32[8192]{0:T(1024)S(1)} all-reduce(f32[8192]{0:T(1024)S(1)} %bitcast.508), channel_id=1, replica_groups=mesh['rows'=4,'cols'=8] {'rows'}, use_global_device_ids=true, to_apply=%region_1.2 | all-reduce | flops 8192 | bytes 65536 | tf_op jit(solution)/shard_map/psum | solution.py:54
  48.0 40.4 %psum.15 = f32[33,33]{1,0:T(8,128)S(1)} all-reduce(f32[33,33]{1,0:T(8,128)S(1)} %fusion.96), channel_id=1, replica_groups=mesh['rows'=4,'cols'=8] {'rows','cols'}, use_global_device_ids=true, to_apply=%region_2.3 | all-reduce | flops 1089 | bytes 8712 | tf_op jit(solution)/shard_map/psum | solution.py:61
  89.1 0.7 fusion.48
  90.5 0.7 fusion.49
  93.3 0.8 fusion.51
  94.8 0.7 fusion.52
  96.2 0.8 fusion.53
  97.7 0.7 fusion.56
  99.1 0.7 fusion.54
  100.5 0.8 fusion.55
  102.0 0.8 fusion.57
  103.4 0.7 fusion.60
  104.9 0.7 fusion.58
  106.3 0.8 fusion.59
  107.7 0.8 fusion.61
  112.0 0.8 fusion.63
  113.5 0.8 fusion.65
  114.9 0.7 fusion.68
  116.3 0.7 fusion.66
  117.8 0.8 fusion.67
  119.2 0.8 fusion.69
  120.6 0.7 fusion.72
  123.5 0.8 fusion.71
  125.0 0.8 fusion.73
  129.3 0.8 fusion.75
  130.7 0.8 fusion.77
  133.6 0.8 fusion.79
  135.0 0.8 fusion.121
  137.3 0.8 fusion.80
  138.7 0.8 fusion.81
  140.1 0.8 fusion.82
  141.5 0.8 fusion.83
  143.0 0.8 fusion.84
  144.4 0.8 fusion.85
  145.9 0.8 fusion.86
  147.3 0.8 fusion.87
  148.8 0.8 fusion.88
  150.2 0.8 fusion.89
  151.7 0.8 fusion.90
  153.1 0.8 fusion.91
  154.6 0.8 fusion.92
  156.0 0.8 fusion.93
  157.4 0.8 fusion.94
  158.8 0.8 fusion.95
  (40 shorter events, 7.7 us)
Async XLA Ops:
  1.4 30.8 %copy-start.4 = (s32[512]{0:T(512)S(1)}, s32[512]{0:T(512)}, u32[]{:S(2)}) copy-start(s32[512]{0:T(512)} %param.7) | copy-start | bytes 6148
  32.3 15.1 %copy-start.2 = (f32[8192]{0:T(1024)S(1)}, f32[8192]{0:T(1024)}, u32[]{:S(2)}) copy-start(f32[8192]{0:T(1024)} %param.8) | copy-start | bytes 98308
  32.3 15.1 %copy-start = (f32[16,8192]{1,0:T(8,128)S(1)}, f32[16,8192]{1,0:T(8,128)}, u32[]{:S(2)}) copy-start(f32[16,8192]{1,0:T(8,128)} %param.10) | copy-start | bytes 1572868
  32.3 15.1 %copy-start.1 = (f32[16,8192]{1,0:T(8,128)S(1)}, f32[16,8192]{1,0:T(8,128)}, u32[]{:S(2)}) copy-start(f32[16,8192]{1,0:T(8,128)} %param.9) | copy-start | bytes 1572868
  47.4 112.8 %copy-start.3 = (f32[8192]{0:T(1024)}, f32[8192]{0:T(1024)S(1)}, u32[]{:S(2)}) copy-start(f32[8192]{0:T(1024)S(1)} %multiply_add_fusion) | copy-start | bytes 98308
